TPU v7x, 512 devices: a whole 4x8x8 slice. The times are simulated.
512 devices in a mesh: bank: 64 (over z, x, core), zero: 8 (over y).
Axes of the slice: x: 4, y: 8, z: 8, core: 2. Of those that a mesh axis runs over, the one named last changes fastest.
Arguments:
- master_down: float32 [64, 1408, 2048], P('bank', None, 'zero'), may hold values from -0.21875 to 0.21875
- second_down: bfloat16 [64, 1408, 2048], P('bank', None, 'zero'), may hold values from -0.078125 to 0.078125
- router_weight: float32 [2048, 64], P('zero', 'bank'), may hold values from -0.125 to 0.125
- router_gain: float32 [2048], P('zero'), may hold values from 0.25 to 1.75
Outputs:
- final_down: bfloat16 [64, 1408, 2048], P('bank')
- scale_down: float32 [64, 1408], P('bank')
- serve_router: bfloat16 [2048, 64], replicated
All inputs are finite; a program needn't handle non-finite values.
Results may differ from a plain program's by a relative error of at most 0.001.
Values may be sent and summed in bfloat16 or wider, within the bound.
A program may use at most 64 MiB of HBM per device.

v0:
```python
import jax
import jax.numpy as jnp
from jax import lax
from jax.sharding import PartitionSpec as P


def from_everyone(value, axis):
    size = lax.axis_size(axis)
    return lax.all_to_all(
        jnp.broadcast_to(value[None], (size, *value.shape)), axis, 0, 0, tiled=True
    )


def over_copies(value, axis):
    return from_everyone(value, axis).sum(axis=0)


def in_order(pieces, dim):
    dims = list(pieces.shape[1:])
    dims[dim] *= pieces.shape[0]
    return jnp.moveaxis(pieces, 0, dim).reshape(dims)


def collect(value, axis, dim):
    return in_order(from_everyone(value, axis), dim)


def body(master_down, second_down, router_weight, router_gain):
    merged_down = master_down + second_down.astype(jnp.float32)
    total_down = over_copies(jnp.sum(merged_down * merged_down, axis=2), "zero")
    scale_down = jnp.sqrt(total_down)
    narrow_down = (merged_down / jnp.expand_dims(scale_down, 2)).astype(jnp.bfloat16)
    final_down = lax.all_gather(narrow_down, "zero", axis=2, tiled=True)
    part_router = (router_weight * router_gain[:, None]).astype(jnp.bfloat16)
    row_router = lax.all_gather(part_router, "zero", axis=0, tiled=True)
    serve_router = collect(row_router, "bank", 1)
    return (final_down, scale_down, serve_router)


def solution(mesh):
    return jax.shard_map(
        body,
        mesh=mesh,
        in_specs=(P("bank", None, "zero"), P("bank", None, "zero"), P("zero", "bank"), P("zero")),
        out_specs=(P("bank", None, None), P("bank", None), P()),
        check_vma=False,
    )
```

profile of v0, /device:TPU:2, one launch (start us, length us, event | category | flops | bytes accessed | tf_op | source)
XLA Modules:
  0.0 115.2 jit_solution(9346307011874724087)
XLA Ops:
  7.2 0.0 copy-start
  7.2 0.0 copy-start.1
  7.2 0.0 all-gather.2.cloned.1.call-start
  7.2 2.0 %multiply_reduce_fusion = f32[1408]{0:T(1024)S(1)} fusion(f32[1,1408,256]{2,1,0:T(8,128)} %param.4, bf16[1,1408,256]{2,1,0:T(8,128)(2,1)} %param.5), kind=kLoop, calls=%fused_computation.1 | loop fusion | flops 1440384 | bytes 2168320 | tf_op jit(solution)/shard_map/reduce_sum | solution.py:30
  9.2 15.1 %all_to_all.10 = f32[8,1,1408]{2,1,0:T(1,128)S(1)} all-to-all(f32[8,1,1408]{2,1,0:T(1,128)S(1)} %broadcast_in_dim.8), channel_id=1, replica_groups=mesh['bank'=64,'zero'=8] {'zero'}, dimensions={0} | all-to-all | bytes 90112 | tf_op jit(solution)/shard_map/all_to_all | solution.py:9
  24.3 0.0 copy-done
  24.4 0.0 copy-done.1
  24.4 0.0 copy-start.2
  24.4 0.0 copy-start.3
  24.4 1.1 divide_convert_fusion
  25.5 0.0 all-gather.2.cloned.1.call-update
  25.5 0.0 copy-done.2
  25.5 0.0 copy-done.3
  25.6 13.9 %all_gather.7 = bf16[2048,1]{0,1:T(2,128)(2,1)S(1)} all-gather(bf16[256,1]{0,1:T(2,128)(2,1)S(1)} %multiply_convert_fusion), channel_id=1, replica_groups=mesh['bank'=64,'zero'=8] {'zero'}, dimensions={0}, use_global_device_ids=true | all-gather | bytes 4608 | tf_op jit(solution)/shard_map/all_gather | solution.py:35
  39.5 0.3 broadcast_bitcast_fusion
  39.8 0.5 broadcast.5
  40.3 2.2 %reduce.3 = bf16[64,2048]{1,0:T(8,128)(2,1)S(1)} reduce(bf16[64,1,2048]{2,1,0:T(2,128)(2,1)S(1)} %broadcast_bitcast_fusion, bf16[]{:T(256)} %broadcast.5), dimensions={1}, to_apply=%broadcast_bitcast_fusion.reduce_sub_computation | reduce | bytes 524290
  42.4 0.9 reshape.35
  43.3 14.0 %all-to-all-start.1 = ((bf16[64,2,1024]{2,1,0:T(2,128)(2,1)}), bf16[64,2,1024]{2,1,0:T(2,128)(2,1)S(1)}, u32[]{:S(2)}, u32[]{:S(2)}) async-start(bf16[64,2,1024]{2,1,0:T(2,128)(2,1)} %reshape.35), calls=%async_computation.1 | async-start | bytes 524288 | tf_op jit(solution)/shard_map/all_to_all | solution.py:9
  57.3 0.6 sqrt.19
  57.9 11.6 %all-to-all-done.1 = bf16[64,2,1024]{2,1,0:T(2,128)(2,1)S(1)} async-done(((bf16[64,2,1024]{2,1,0:T(2,128)(2,1)}), bf16[64,2,1024]{2,1,0:T(2,128)(2,1)S(1)}, u32[]{:S(2)}, u32[]{:S(2)}) %all-to-all-start.1) | async-done | bytes 262176 | tf_op jit(solution)/shard_map/all_to_all | solution.py:9
  69.5 0.2 reshape.36
  69.8 0.9 copy.13
  70.6 31.6 %all-gather.2.cloned.1.call-done = bf16[1,1408,2048]{2,1,0:T(8,128)(2,1)} async-done(((bf16[1,1408,256]{2,1,0:T(8,128)(2,1)}), bf16[1,1408,2048]{2,1,0:T(8,128)(2,1)}) %all-gather.2.cloned.1.call-update) | async-done | bytes 5767184 | tf_op jit(solution)/shard_map/all_gather | solution.py:33
  102.2 6.2 %copy.15 = bf16[1,1408,2048]{2,1,0:T(8,128)(2,1)} copy(bf16[1,1408,2048]{2,1,0:T(8,128)(2,1)} %all-gather.2.cloned.1.call-done) | data formatting | bytes 11534336
  (5 shorter events, 0.1 us)
Async XLA Ops:
  7.2 17.2 %copy-start = (f32[1,1408,256]{2,1,0:T(8,128)S(1)}, f32[1,1408,256]{2,1,0:T(8,128)}, u32[]{:S(2)}) copy-start(f32[1,1408,256]{2,1,0:T(8,128)} %param.4) | copy-start | bytes 4325380
  7.2 17.2 %copy-start.1 = (bf16[1,1408,256]{2,1,0:T(8,128)(2,1)S(1)}, bf16[1,1408,256]{2,1,0:T(8,128)(2,1)}, u32[]{:S(2)}) copy-start(bf16[1,1408,256]{2,1,0:T(8,128)(2,1)} %param.5) | copy-start | bytes 2162692
  7.2 95.0 %all-gather.2.cloned.1.call-start = ((), (), s32[]{:S(2)}) async-start(), calls=%async_computation.2 | async-start | bytes 6488064 | tf_op jit(solution)/shard_map/all_gather | solution.py:33
  24.4 1.2 %copy-start.2 = (f32[256,1]{0,1:T(1,128)S(1)}, f32[256,1]{0,1:T(1,128)}, u32[]{:S(2)}) copy-start(f32[256,1]{0,1:T(1,128)} %param.6) | copy-start | bytes 3076
  24.4 1.2 %copy-start.3 = (f32[256]{0:T(256)S(1)}, f32[256]{0:T(256)}, u32[]{:S(2)}) copy-start(f32[256]{0:T(256)} %param.7) | copy-start | bytes 3076
  43.3 26.2 %all-to-all-start.1 = ((bf16[64,2,1024]{2,1,0:T(2,128)(2,1)}), bf16[64,2,1024]{2,1,0:T(2,128)(2,1)S(1)}, u32[]{:S(2)}, u32[]{:S(2)}) async-start(bf16[64,2,1024]{2,1,0:T(2,128)(2,1)} %reshape.35), calls=%async_computation.1 | async-start | bytes 524288 | tf_op jit(solution)/shard_map/all_to_all | solution.py:9
Sparse Core Ops, SparseCore 0:
  25.6 76.5 all-gather.1
where the time goes:
time: 115 us
  waiting for transfers between devices  43.2 us (38%)
  blocking collectives  28.9 us (25%)
  starting transfers between devices  14.1 us (12%)
  between operations  14.1 us (12%)
  local copies, waits for them, and re-layouts  9.55 us (8%)
  other arithmetic  5.32 us (5%)
    all_gather x1, waiting for transfers between devices, body(): final_down = lax.all_gather(narrow_down, 'zero', axis=2, tiled=True)  31.6 us
    all_to_all x1, blocking collectives, from_everyone(): lax.all_to_all(jnp.broadcast_to(value[None], (size, *value.shape)), axis,...  15.1 us
    all_to_all x1, starting transfers between devices, from_everyone(): lax.all_to_all(jnp.broadcast_to(value[None], (size, *value.shape)), axis,...  14 us
    all_gather x1, blocking collectives, body(): row_router = lax.all_gather(part_router, 'zero', axis=0, tiled=True)  13.9 us
    all_to_all x1, waiting for transfers between devices, from_everyone(): lax.all_to_all(jnp.broadcast_to(value[None], (size, *value.shape)), axis,...  11.6 us
    unnamed x13, local copies, waits for them, and re-layouts  8.07 us
  transfers between devices with their start and end apart: 2, of which 2 were waited for; matrix products, arithmetic and copies ran while one was open for 5% of the time, Pallas kernels for 0%

commit v1 on v0

--- a/solution.py
+++ b/solution.py
@@ -1,7 +1,18 @@
+import functools
 import jax
 import jax.numpy as jnp
 from jax import lax
 from jax.sharding import PartitionSpec as P
+
+
+def prepare_tracks(arr_in, axis_name):
+    degree = lax.axis_size(axis_name)
+    aux = tuple((degree if u == 2 else 1 for u in range(arr_in.ndim)))
+    mixed_arr = jnp.tile(arr_in, aux)
+    return lax.all_to_all(mixed_arr, axis_name, split_axis=2, concat_axis=2, tiled=True)
+
+
+_prepare_leaves = functools.partial(prepare_tracks, axis_name="zero")
 
 
 def from_everyone(value, axis):
@@ -30,7 +41,7 @@
     total_down = over_copies(jnp.sum(merged_down * merged_down, axis=2), "zero")
     scale_down = jnp.sqrt(total_down)
     narrow_down = (merged_down / jnp.expand_dims(scale_down, 2)).astype(jnp.bfloat16)
-    final_down = lax.all_gather(narrow_down, "zero", axis=2, tiled=True)
+    final_down = _prepare_leaves(narrow_down)
     part_router = (router_weight * router_gain[:, None]).astype(jnp.bfloat16)
     row_router = lax.all_gather(part_router, "zero", axis=0, tiled=True)
     serve_router = collect(row_router, "bank", 1)

time: 115 us -> 460 us (4.00)
  local copies, waits for them, and re-layouts: 9.55 us -> 158 us
  other arithmetic: 5.32 us -> 129 us
  waiting for transfers between devices: 43.2 us -> 129 us
  between operations: 14.1 us -> 0.77 us
  blocking collectives: 28.9 us -> 16.5 us
  starting transfers between devices: 14.1 us -> 25.8 us
    all_to_all x0 -> x1, waiting for transfers between devices: none -> 129 us  [prepare_tracks(): lax.all_to_all(mixed_arr, axis_name, split_axis=2, concat_axis=2, tiled=T...]
    unnamed x1 -> x2, other arithmetic: 2.15 us -> 126 us
    another operation x0 -> x3, local copies, waits for them, and re-layouts: none -> 109 us  [prepare_tracks(): mixed_arr = jnp.tile(arr_in, aux)]
    unnamed x13 -> x15, local copies, waits for them, and re-layouts: 8.07 us -> 47.2 us
    all_gather x1 -> x0, waiting for transfers between devices: 31.6 us -> none  [body(): final_down = lax.all_gather(narrow_down, 'zero', axis=2, tiled=True)]
    all_to_all x1 -> x0, blocking collectives: 15.1 us -> none  [from_everyone(): lax.all_to_all(jnp.broadcast_to(value[None], (size, *value.shape)), axis,...]
    all_to_all x1 -> x2, waiting for transfers between devices: 11.6 us -> 0.01 us  [from_everyone(): lax.all_to_all(jnp.broadcast_to(value[None], (size, *value.shape)), axis,...]
    all_to_all x1 -> x2, starting transfers between devices: 14 us -> 21.1 us  [from_everyone(): lax.all_to_all(jnp.broadcast_to(value[None], (size, *value.shape)), axis,...]
  transfers between devices with their start and end apart: 2 -> 3, of which waited for: 2 -> 1; matrix products, arithmetic and copies ran while one was open for 5% -> 54% of each run, Pallas kernels for 0% -> 0%
where the time goes in v1:
time: 460 us; the launch traced here: 459 us
  local copies, waits for them, and re-layouts  158 us (34%)
  other arithmetic  129 us (28%)
  waiting for transfers between devices  129 us (28%)
  starting transfers between devices  25.8 us (6%)
  blocking collectives  16.5 us (4%)
    all_to_all x1, waiting for transfers between devices, prepare_tracks(): lax.all_to_all(mixed_arr, axis_name, split_axis=2, concat_axis=2, tiled=T...  129 us
    unnamed x2, other arithmetic  126 us
    another operation x3, local copies, waits for them, and re-layouts, prepare_tracks(): mixed_arr = jnp.tile(arr_in, aux)  109 us
    unnamed x15, local copies, waits for them, and re-layouts  47.2 us
    all_to_all x2, starting transfers between devices, from_everyone(): lax.all_to_all(jnp.broadcast_to(value[None], (size, *value.shape)), axis,...  21.1 us
    all_gather x1, blocking collectives, body(): row_router = lax.all_gather(part_router, 'zero', axis=0, tiled=True)  16.5 us
  transfers between devices with their start and end apart: 3, of which 1 were waited for; matrix products, arithmetic and copies ran while one was open for 54% of the time, Pallas kernels for 0%

profile of v1, /device:TPU:2, one launch (start us, length us, event | category | flops | bytes accessed | tf_op | source)
XLA Modules:
  0.0 458.8 jit_solution(17480194419158915375)
XLA Ops:
  0.6 0.0 copy-start.3
  0.6 0.0 copy-start.2
  0.7 1.8 multiply_reduce_fusion
  2.5 0.0 copy-start
  2.5 0.0 copy-start.1
  2.5 0.6 broadcast_in_dim.8
  3.1 7.2 %all-to-all-start = ((f32[8,1,1408]{2,1,0:T(1,128)}), f32[8,1,1408]{2,1,0:T(1,128)S(1)}, u32[]{:S(2)}, u32[]{:S(2)}) async-start(f32[8,1,1408]{2,1,0:T(1,128)} %broadcast_in_dim.8), calls=%async_computation | async-start | bytes 90112 | tf_op jit(solution)/shard_map/all_to_all | solution.py:20
  10.4 0.0 copy-done.3
  10.4 0.0 copy-done.2
  10.4 16.5 %all_gather.3 = bf16[2048,1]{0,1:T(2,128)(2,1)S(1)} all-gather(bf16[256,1]{0,1:T(2,128)(2,1)S(1)} %multiply_convert_fusion), channel_id=1, replica_groups=mesh['bank'=64,'zero'=8] {'zero'}, dimensions={0}, use_global_device_ids=true | all-gather | bytes 4608 | tf_op jit(solution)/shard_map/all_gather | solution.py:46
  27.0 0.3 broadcast_bitcast_fusion
  27.3 0.5 broadcast.8
  27.8 2.2 reduce.4
  29.9 0.9 reshape.43
  30.8 0.0 all-to-all-done
  30.8 13.9 %all-to-all-start.2 = ((bf16[64,2,1024]{2,1,0:T(2,128)(2,1)}), bf16[64,2,1024]{2,1,0:T(2,128)(2,1)S(1)}, u32[]{:S(2)}, u32[]{:S(2)}) async-start(bf16[64,2,1024]{2,1,0:T(2,128)(2,1)} %reshape.43), calls=%async_computation.2 | async-start | bytes 524288 | tf_op jit(solution)/shard_map/all_to_all | solution.py:20
  44.8 0.0 copy-done
  44.8 0.0 copy-done.1
  44.8 0.3 fusion
  45.1 0.3 copy.18
  45.4 0.4 tile.12
  45.8 108.2 %copy.26 = bf16[1,1408,2048]{1,0,2:T(2,128)(2,1)} copy(bf16[1,1408,2048]{1,2,0:T(8,128)(2,1)S(1)} %bitcast.18) | data formatting | bytes 11534336 | tf_op jit(solution)/shard_map/tile | solution.py:11
  154.0 124.2 %reduce.3 = bf16[2048,1408]{1,0:T(8,128)(2,1)} reduce(bf16[2048,1,1408]{2,1,0:T(2,128)(2,1)} %bitcast.16, bf16[]{:T(256)} %broadcast.8), dimensions={1}, to_apply=%bitcast.15.reduce_sub_computation | reduce | bytes 11534338
  278.2 8.1 %reshape.41 = bf16[8,2,180224]{2,1,0:T(2,128)(2,1)} reshape(bf16[2048,1408]{1,0:T(8,128)(2,1)} %reduce.3) | data formatting | bytes 11534336
  286.3 0.0 all-to-all-done.2
  286.3 4.7 %all-to-all-start.1 = ((bf16[8,2,180224]{2,1,0:T(2,128)(2,1)}), bf16[8,2,180224]{2,1,0:T(2,128)(2,1)}, u32[]{:S(2)}, u32[]{:S(2)}) async-start(bf16[8,2,180224]{2,1,0:T(2,128)(2,1)} %reshape.41), calls=%async_computation.1 | async-start | bytes 11534336 | tf_op jit(solution)/shard_map/all_to_all | solution.py:12
  291.0 0.6 sqrt.19
  291.6 0.2 reshape.44
  291.8 0.9 copy.25
  292.7 128.9 %all-to-all-done.1 = bf16[8,2,180224]{2,1,0:T(2,128)(2,1)} async-done(((bf16[8,2,180224]{2,1,0:T(2,128)(2,1)}), bf16[8,2,180224]{2,1,0:T(2,128)(2,1)}, u32[]{:S(2)}, u32[]{:S(2)}) %all-to-all-start.1) | async-done | bytes 5767200 | tf_op jit(solution)/shard_map/all_to_all | solution.py:12
  421.6 10.4 %reshape.42 = bf16[2048,1,1408]{2,1,0:T(2,128)(2,1)} reshape(bf16[8,2,180224]{2,1,0:T(2,128)(2,1)} %all-to-all-done.1) | data formatting | bytes 11534336
  432.0 26.9 %copy.21 = bf16[1,1408,2048]{2,1,0:T(8,128)(2,1)} copy(bf16[1,1408,2048]{1,0,2:T(2,128)(2,1)} %bitcast.17) | data formatting | bytes 11534336
  (4 shorter events, 0.1 us)
Async XLA Ops:
  0.6 9.8 %copy-start.3 = (f32[256]{0:T(256)S(1)}, f32[256]{0:T(256)}, u32[]{:S(2)}) copy-start(f32[256]{0:T(256)} %param.7) | copy-start | bytes 3076
  0.6 9.8 %copy-start.2 = (f32[256,1]{0,1:T(1,128)S(1)}, f32[256,1]{0,1:T(1,128)}, u32[]{:S(2)}) copy-start(f32[256,1]{0,1:T(1,128)} %param.6) | copy-start | bytes 3076
  2.5 42.3 %copy-start = (f32[1,1408,256]{2,1,0:T(8,128)S(1)}, f32[1,1408,256]{2,1,0:T(8,128)}, u32[]{:S(2)}) copy-start(f32[1,1408,256]{2,1,0:T(8,128)} %param.4) | copy-start | bytes 4325380
  2.5 42.3 %copy-start.1 = (bf16[1,1408,256]{2,1,0:T(8,128)(2,1)S(1)}, bf16[1,1408,256]{2,1,0:T(8,128)(2,1)}, u32[]{:S(2)}) copy-start(bf16[1,1408,256]{2,1,0:T(8,128)(2,1)} %param.5) | copy-start | bytes 2162692
  3.1 27.7 %all-to-all-start = ((f32[8,1,1408]{2,1,0:T(1,128)}), f32[8,1,1408]{2,1,0:T(1,128)S(1)}, u32[]{:S(2)}, u32[]{:S(2)}) async-start(f32[8,1,1408]{2,1,0:T(1,128)} %broadcast_in_dim.8), calls=%async_computation | async-start | bytes 90112 | tf_op jit(solution)/shard_map/all_to_all | solution.py:20
  30.8 255.5 %all-to-all-start.2 = ((bf16[64,2,1024]{2,1,0:T(2,128)(2,1)}), bf16[64,2,1024]{2,1,0:T(2,128)(2,1)S(1)}, u32[]{:S(2)}, u32[]{:S(2)}) async-start(bf16[64,2,1024]{2,1,0:T(2,128)(2,1)} %reshape.43), calls=%async_computation.2 | async-start | bytes 524288 | tf_op jit(solution)/shard_map/all_to_all | solution.py:20
  286.3 135.3 %all-to-all-start.1 = ((bf16[8,2,180224]{2,1,0:T(2,128)(2,1)}), bf16[8,2,180224]{2,1,0:T(2,128)(2,1)}, u32[]{:S(2)}, u32[]{:S(2)}) async-start(bf16[8,2,180224]{2,1,0:T(2,128)(2,1)} %reshape.41), calls=%async_computation.1 | async-start | bytes 11534336 | tf_op jit(solution)/shard_map/all_to_all | solution.py:12
